TPU v7x, 32 devices: a 4x4x1 block of a 4x4x8 slice. The times are simulated.
32 devices in a mesh: rep: 1 (over z), r: 4 (over y), s: 8 (over x, core).
Axes of the slice: x: 4, y: 4, z: 1, core: 2. Of those that a mesh axis runs over, the one named last changes fastest.
The devices are a block of a 4x4x8 slice.
Arguments:
- x: bfloat16 [32, 2048, 1024], P(('rep', 'r', 's'))
- dy: bfloat16 [32, 2048, 1024], P(('rep', 'r', 's'))
- w_gate: bfloat16 [2, 1024, 2560], P(None, 's')
- w_up: bfloat16 [2, 1024, 2560], P(None, 's')
- w_down: bfloat16 [2, 2560, 1024], P(None, 's')
Outputs:
- output 1: bfloat16 [32, 2048, 1024], P(('rep', 'r', 's'))
- output 2: bfloat16 [2, 1024, 2560], P('rep', 's')
- output 3: bfloat16 [2, 1024, 2560], P('rep', 's')
- output 4: bfloat16 [2, 2560, 1024], P('rep', 's')
All inputs are finite; a program needn't handle non-finite values.
Results may differ from a plain program's by a relative error of at most 0.018.
Values are sent between devices in bfloat16 or wider.
A program may use at most 768 MiB of HBM per device.

v0:
```python
import jax
import jax.numpy as jnp
from jax import lax
from jax.sharding import PartitionSpec as P

NAMES = ("w_gate", "w_up", "w_down")


def matmul(a, w):
    return jnp.dot(a, w, preferred_element_type=jnp.float32).astype(jnp.bfloat16)


def normed(h):
    wide = h.astype(jnp.float32)
    scale = lax.rsqrt(jnp.mean(wide**2, -1, keepdims=True) + 1e-6)
    return (wide * scale).astype(jnp.bfloat16)


def layer(h, w):
    a = normed(h)
    gate = jnp.dot(a, w["w_gate"], preferred_element_type=jnp.float32)
    up = jnp.dot(a, w["w_up"], preferred_element_type=jnp.float32)
    return h + matmul((jax.nn.silu(gate) * up).astype(jnp.bfloat16), w["w_down"])


def solution(mesh):
    def fetched(weights, number):
        return {name: lax.all_gather(w[number], "s", axis=0, tiled=True) for name, w in zip(NAMES, weights, strict=True)}

    def summed(term):
        return lax.psum(lax.psum_scatter(term, "s", scatter_dimension=0, tiled=True), "r")

    def step(x, dy, *weights):
        layers = weights[0].shape[0]
        h, inputs = x[0], []
        for number in range(layers):
            inputs.append(h)
            h = layer(h, fetched(weights, number))
        by_h, mine = dy[0], [None] * layers
        for number in reversed(range(layers)):
            _, back = jax.vjp(lambda w, h: layer(h, w), fetched(weights, number), inputs[number])
            by_w, by_h = back(by_h)
            mine[number] = [summed(by_w[name]) for name in NAMES]
        return (by_h[None], *(jnp.stack([mine[number][i] for number in range(layers)]) for i in range(3)))

    states, cut = P(("rep", "r", "s"), None, None), P(None, "s", None)
    return jax.shard_map(
        step,
        mesh=mesh,
        in_specs=(states, states) + (cut,) * 3,
        out_specs=(states,) + (P("rep", "s", None),) * 3,
        check_vma=False,
    )
```

profile of v0, /device:TPU:97, one launch (start us, length us, event | category | flops | bytes accessed | tf_op | source)
XLA Modules:
  0.0 647.4 jit_solution(4053667001952005254)
XLA Ops:
  17.0 6.4 copy.10
  27.1 6.5 %copy.9 = bf16[1,2048,1024]{1,2,0:T(8,128)(2,1)} copy(bf16[1,2048,1024]{2,1,0:T(8,128)(2,1)} %param.6) | data formatting | bytes 8388608 | tf_op args[1]
  33.6 14.5 %all-gather.13.cloned.1.call-done = bf16[1,1024,2560]{2,1,0:T(8,128)(2,1)} async-done(((bf16[1,128,2560]{2,1,0:T(8,128)(2,1)}), bf16[1,1024,2560]{2,1,0:T(8,128)(2,1)}) %all-gather.13.cloned.1.call-update) | async-done | bytes 5242896 | tf_op jit(solution)/shard_map/all_gather | solution.py:28
  48.1 18.2 %fusion.40 = f32[2048,2560]{1,0:T(8,128)} fusion(bf16[1,1024,2560]{2,1,0:T(8,128)(2,1)} %all-gather.13.cloned.1.call-done, bf16[1,2048,1024]{1,2,0:T(8,128)(2,1)} %copy.10, f32[2048]{0:T(1024)S(1)} %fusion.61), kind=kOutput, calls=%fused_computation.65 | convolution fusion | flops 10743709696 | bytes 30416896 | tf_op jit(solution)/shard_map/dot_general | solution.py:21
  66.4 17.1 %all-gather.15.cloned.1.call-done = bf16[1,1024,2560]{2,1,0:T(8,128)(2,1)} async-done(((bf16[1,128,2560]{2,1,0:T(8,128)(2,1)}), bf16[1,1024,2560]{2,1,0:T(8,128)(2,1)}) %all-gather.15.cloned.1.call-update) | async-done | bytes 5242896 | tf_op jit(solution)/shard_map/all_gather | solution.py:28
  83.4 28.7 %multiply_convert_fusion.1 = (bf16[2048,2560]{1,0:T(8,128)(2,1)}, f32[2048,2560]{1,0:T(8,128)}) fusion(f32[2048,2560]{1,0:T(8,128)} %fusion.40, bf16[1,1024,2560]{2,1,0:T(8,128)(2,1)} %all-gather.15.cloned.1.call-done, bf16[1,2048,1024]{1,2,0:T(8,128)(2,1)} %copy.10, f32[2048]{0:T(1024)S(1)} %fusion.61), kind=kOutput, calls=%fused_computation.13 | convolution fusion | flops 10775166976 | bytes 61874176 | tf_op jit(solution)/shard_map/dot_general | solution.py:22
  112.1 6.7 %all-gather.17.cloned.1.call-done = bf16[1,2560,1024]{2,1,0:T(8,128)(2,1)} async-done(((bf16[1,320,1024]{2,1,0:T(8,128)(2,1)}), bf16[1,2560,1024]{2,1,0:T(8,128)(2,1)}) %all-gather.17.cloned.1.call-update) | async-done | bytes 5242896 | tf_op jit(solution)/shard_map/all_gather | solution.py:28
  118.8 17.9 %fusion.18 = (f32[2048]{0:T(1024)S(1)}, bf16[2048,1024]{0,1:T(8,128)(2,1)}) fusion(bf16[2048,2560]{1,0:T(8,128)(2,1)} %get-tuple-element.20, bf16[1,2560,1024]{2,1,0:T(8,128)(2,1)} %all-gather.17.cloned.1.call-done, bf16[1,2048,1024]{1,2,0:T(8,128)(2,1)} %copy.10), kind=kOutput, calls=%fused_computation.40 | convolution fusion | flops 10747901952 | bytes 24125440 | tf_op jit(solution)/shard_map/dot_general | solution.py:10
  137.2 16.7 %all-gather.21.cloned.1.call-done = bf16[1,2560,1024]{2,1,0:T(8,128)(2,1)} async-done(((bf16[1,320,1024]{2,1,0:T(8,128)(2,1)}), bf16[1,2560,1024]{2,1,0:T(8,128)(2,1)}) %all-gather.21.cloned.1.call-update) | async-done | bytes 5242896 | tf_op jit(solution)/shard_map/all_gather | solution.py:28
  153.9 17.2 %convolution_convert_fusion.1 = bf16[2048,2560]{1,0:T(8,128)(2,1)} fusion(bf16[1,2560,1024]{2,1,0:T(8,128)(2,1)} %all-gather.21.cloned.1.call-done, bf16[1,2048,1024]{2,1,0:T(8,128)(2,1)} %param.6), kind=kOutput, calls=%fused_computation.29 | convolution fusion | flops 10742661120 | bytes 19922944 | tf_op jit(solution)/shard_map/transpose(jvp())/dot_general | solution.py:10
  171.2 18.5 %all-gather.23.cloned.1.call-done = bf16[1,1024,2560]{2,1,0:T(8,128)(2,1)} async-done(((bf16[1,128,2560]{2,1,0:T(8,128)(2,1)}), bf16[1,1024,2560]{2,1,0:T(8,128)(2,1)}) %all-gather.23.cloned.1.call-update) | async-done | bytes 5242896 | tf_op jit(solution)/shard_map/all_gather | solution.py:28
  189.7 18.3 %fusion.24 = f32[2048,2560]{1,0:T(8,128)} fusion(bf16[1,1024,2560]{2,1,0:T(8,128)(2,1)} %all-gather.23.cloned.1.call-done, bf16[2048,1024]{0,1:T(8,128)(2,1)} %get-tuple-element.23, f32[2048]{0:T(1024)S(1)} %fusion.62), kind=kOutput, calls=%fused_computation.49 | convolution fusion | flops 10743709696 | bytes 30416896 | tf_op jit(solution)/shard_map/jvp()/dot_general | solution.py:22
  208.0 17.4 %all-gather.19.cloned.1.call-done = bf16[1,1024,2560]{2,1,0:T(8,128)(2,1)} async-done(((bf16[1,128,2560]{2,1,0:T(8,128)(2,1)}), bf16[1,1024,2560]{2,1,0:T(8,128)(2,1)}) %all-gather.19.cloned.1.call-update) | async-done | bytes 5242896 | tf_op jit(solution)/shard_map/all_gather | solution.py:28
  225.4 32.0 %fusion.1 = (bf16[2048,2560]{1,0:T(8,128)(2,1)}, f32[2048,2560]{1,0:T(8,128)}) fusion(f32[2048,2560]{1,0:T(8,128)} %fusion.24, bf16[2048,2560]{1,0:T(8,128)(2,1)} %convolution_convert_fusion.1, bf16[1,1024,2560]{2,1,0:T(8,128)(2,1)} %all-gather.19.cloned.1.call-done, bf16[2048,1024]{0,1:T(8,128)(2,1)} %get-tuple-element.23, f32[2048]{0:T(1024)S(1)} %fusion.62), kind=kOutput, calls=%fused_computation.7 | convolution fusion | flops 10806624256 | bytes 72359936 | tf_op jit(solution)/shard_map/jvp()/dot_general | solution.py:21
  257.4 20.0 %fusion.7 = bf16[2048,1024]{0,1:T(8,128)(2,1)} fusion(bf16[2048,2560]{1,0:T(8,128)(2,1)} %convolution_convert_fusion.1, bf16[1,1024,2560]{2,1,0:T(8,128)(2,1)} %all-gather.23.cloned.1.call-done, f32[2048,2560]{1,0:T(8,128)} %get-tuple-element.25), kind=kOutput, calls=%fused_computation.25 | convolution fusion | flops 10768875520 | bytes 40894464 | tf_op jit(solution)/shard_map/transpose(jvp())/dot_general | solution.py:22
  277.5 17.5 %fusion.20 = (f32[2048]{0:T(1024)S(1)}, bf16[2048,1024]{0,1:T(8,128)(2,1)S(1)}) fusion(bf16[2048,1024]{0,1:T(8,128)(2,1)} %get-tuple-element.23, bf16[2048,1024]{0,1:T(8,128)(2,1)} %fusion.7, bf16[2048,2560]{1,0:T(8,128)(2,1)} %get-tuple-element.24, bf16[1,1024,2560]{2,1,0:T(8,128)(2,1)} %all-gather.19.cloned.1.call-done), kind=kOutput, calls=%fused_computation.42 | convolution fusion | flops 10747901952 | bytes 28319744 | tf_op jit(solution)/shard_map/transpose(jvp())/dot_general | solution.py:21
  295.0 3.6 fusion.44
  300.6 15.8 %convolution_convert_fusion.2 = bf16[2560,1024]{1,0:T(8,128)(2,1)} fusion(bf16[2048,2560]{1,0:T(8,128)(2,1)} %get-tuple-element.20, bf16[2048,1024]{0,1:T(8,128)(2,1)S(1)} %fusion.44), kind=kOutput, calls=%fused_computation.46 | convolution fusion | flops 10740039680 | bytes 19922944 | tf_op jit(solution)/shard_map/transpose(jvp())/dot_general | solution.py:10
  316.6 22.0 %fusion.21 = bf16[2560,1024]{1,0:T(8,128)(2,1)} fusion(f32[2048,2560]{1,0:T(8,128)} %fusion.24, bf16[1,2048,1024]{2,1,0:T(8,128)(2,1)} %param.6, f32[2048,2560]{1,0:T(8,128)} %get-tuple-element.25), kind=kOutput, calls=%fused_computation.43 | convolution fusion | flops 10771496960 | bytes 51380224 | tf_op jit(solution)/shard_map/transpose(jvp())/dot_general | solution.py:10
  338.7 31.8 %fusion.3 = (bf16[2048,2560]{1,0:T(8,128)(2,1)}, bf16[2048,2560]{1,0:T(8,128)(2,1)}) fusion(f32[2048,2560]{1,0:T(8,128)} %fusion.40, f32[2048,2560]{1,0:T(8,128)} %get-tuple-element.21, bf16[2048,1024]{0,1:T(8,128)(2,1)} %copy-done.1, bf16[1,2560,1024]{2,1,0:T(8,128)(2,1)} %all-gather.17.cloned.1.call-done), kind=kOutput, calls=%fused_computation.9 | convolution fusion | flops 10805575680 | bytes 72351744 | tf_op jit(solution)/shard_map/transpose(jvp())/dot_general | solution.py:10
  370.6 20.2 %fusion.22 = bf16[1024,2560]{1,0:T(8,128)(2,1)} fusion(bf16[2048,2560]{1,0:T(8,128)(2,1)} %get-tuple-element.29, bf16[1,2048,1024]{1,2,0:T(8,128)(2,1)} %copy.10, f32[2048]{0:T(1024)S(1)} %copy-done.8, f32[2048,2560]{1,0:T(8,128)} %fusion.40), kind=kOutput, calls=%fused_computation.44 | convolution fusion | flops 10777788416 | bytes 40902656 | tf_op jit(solution)/shard_map/transpose(jvp())/dot_general | solution.py:22
  390.9 20.3 %fusion.23 = bf16[1024,2560]{1,0:T(8,128)(2,1)} fusion(bf16[2048,2560]{1,0:T(8,128)(2,1)} %convolution_convert_fusion.1, bf16[2048,1024]{0,1:T(8,128)(2,1)} %get-tuple-element.23, f32[2048]{0:T(1024)S(1)} %copy-done.10, f32[2048,2560]{1,0:T(8,128)} %get-tuple-element.25), kind=kOutput, calls=%fused_computation.45 | convolution fusion | flops 10777788416 | bytes 40902656 | tf_op jit(solution)/shard_map/transpose(jvp())/dot_general | solution.py:22
  411.3 16.5 %convolution_convert_fusion.3 = bf16[1024,2560]{1,0:T(8,128)(2,1)} fusion(bf16[2048,2560]{1,0:T(8,128)(2,1)} %get-tuple-element.24, bf16[2048,1024]{0,1:T(8,128)(2,1)} %get-tuple-element.23, f32[2048]{0:T(1024)S(1)} %copy-done.10), kind=kOutput, calls=%fused_computation.47 | convolution fusion | flops 10743709696 | bytes 19931136 | tf_op jit(solution)/shard_map/transpose(jvp())/dot_general | solution.py:21
  427.9 16.5 %convolution_convert_fusion.4 = bf16[1024,2560]{1,0:T(8,128)(2,1)} fusion(bf16[2048,2560]{1,0:T(8,128)(2,1)} %get-tuple-element.28, bf16[1,2048,1024]{1,2,0:T(8,128)(2,1)} %copy.10, f32[2048]{0:T(1024)S(1)} %copy-done.8), kind=kOutput, calls=%fused_computation.48 | convolution fusion | flops 10743709696 | bytes 19931136 | tf_op jit(solution)/shard_map/transpose(jvp())/dot_general | solution.py:21
  444.5 20.2 %fusion.9 = bf16[2048,1024]{0,1:T(8,128)(2,1)} fusion(bf16[2048,2560]{1,0:T(8,128)(2,1)} %get-tuple-element.29, bf16[1,1024,2560]{2,1,0:T(8,128)(2,1)} %all-gather.15.cloned.1.call-done, f32[2048,2560]{1,0:T(8,128)} %fusion.40), kind=kOutput, calls=%fused_computation.27 | convolution fusion | flops 10768875520 | bytes 40894464 | tf_op jit(solution)/shard_map/transpose(jvp())/dot_general | solution.py:22
  464.8 4.0 reduce-scatter.13.cloned.1.call-done
  468.8 39.2 %reduce-scatter.9.cloned.1.call-done = bf16[128,2560]{1,0:T(8,128)(2,1)} async-done(((bf16[1024,2560]{1,0:T(8,128)(2,1)}), bf16[128,2560]{1,0:T(8,128)(2,1)}) %reduce-scatter.9.cloned.1.call-update) | async-done | bytes 655376 | tf_op jit(solution)/shard_map/reduce_scatter | solution.py:31
  508.0 39.0 %reduce-scatter.7.cloned.1.call-done = bf16[128,2560]{1,0:T(8,128)(2,1)} async-done(((bf16[1024,2560]{1,0:T(8,128)(2,1)}), bf16[128,2560]{1,0:T(8,128)(2,1)}) %reduce-scatter.7.cloned.1.call-update) | async-done | bytes 655376 | tf_op jit(solution)/shard_map/reduce_scatter | solution.py:31
  547.1 17.5 %fusion.17 = (f32[2048]{0:T(1024)S(1)}, bf16[2048,1024]{0,1:T(8,128)(2,1)S(1)}) fusion(bf16[1,2048,1024]{1,2,0:T(8,128)(2,1)} %copy.10, bf16[2048,1024]{0,1:T(8,128)(2,1)} %fusion.9, bf16[2048,2560]{1,0:T(8,128)(2,1)} %get-tuple-element.28, bf16[1,1024,2560]{2,1,0:T(8,128)(2,1)} %all-gather.13.cloned.1.call-done), kind=kOutput, calls=%fused_computation.39 | convolution fusion | flops 10747901952 | bytes 28319744 | tf_op jit(solution)/shard_map/transpose(jvp())/dot_general | solution.py:21
  564.6 4.7 fusion.43
  569.3 6.4 copy.11
  575.7 59.1 %all-reduce.3.cloned.1.call-done = (bf16[1,128,2560]{2,1,0:T(8,128)(2,1)}, bf16[1,128,2560]{2,1,0:T(8,128)(2,1)}, bf16[1,128,2560]{2,1,0:T(8,128)(2,1)}, bf16[1,...) async-done(((bf16[1,128,2560]{2,1,0:T(8,128)(2,1)}, bf16[1,128,2560]{2,1,0:T(8,128)(2,1)}, bf16[1,128,2560]{2,1,0:T(8,128)(2,1)}, ...) | async-done | bytes 3932176 | tf_op jit(solution)/shard_map/psum | solution.py:31
  (65 shorter events, 22.7 us)
Async XLA Ops:
  7.2 40.9 %all-gather.13.cloned.1.call-start = ((), (), s32[]{:S(2)}) async-start(), calls=%async_computation.12 | async-start | bytes 5898240 | tf_op jit(solution)/shard_map/all_gather | solution.py:28
  9.7 73.7 %all-gather.15.cloned.1.call-start = ((), (), s32[]{:S(2)}) async-start(), calls=%async_computation.13 | async-start | bytes 5898240 | tf_op jit(solution)/shard_map/all_gather | solution.py:28
  12.3 106.4 %all-gather.17.cloned.1.call-start = ((), (), s32[]{:S(2)}) async-start(), calls=%async_computation.14 | async-start | bytes 5898240 | tf_op jit(solution)/shard_map/all_gather | solution.py:28
  15.0 138.9 %all-gather.21.cloned.1.call-start = ((), (), s32[]{:S(2)}) async-start(), calls=%async_computation.16 | async-start | bytes 5898240 | tf_op jit(solution)/shard_map/all_gather | solution.py:28
  15.6 174.0 %all-gather.23.cloned.1.call-start = ((), (), s32[]{:S(2)}) async-start(), calls=%async_computation.17 | async-start | bytes 5898240 | tf_op jit(solution)/shard_map/all_gather | solution.py:28
  16.3 209.1 %all-gather.19.cloned.1.call-start = ((), (), s32[]{:S(2)}) async-start(), calls=%async_computation.15 | async-start | bytes 5898240 | tf_op jit(solution)/shard_map/all_gather | solution.py:28
  16.9 447.9 %reduce-scatter.15.cloned.1.call-start = ((), (), s32[]{:S(2)}) async-start(), calls=%async_computation.10 | async-start | bytes 5898240 | tf_op jit(solution)/shard_map/reduce_scatter | solution.py:31
  26.5 0.6 copy-start.5
  27.1 56.3 %copy-start.7 = (f32[2048]{0:T(1024)}, f32[2048]{0:T(1024)S(1)}, u32[]{:S(2)}) copy-start(f32[2048]{0:T(1024)S(1)} %fusion.61) | copy-start | bytes 24580
  136.6 0.6 copy-start.11
  137.2 157.8 %copy-start.9 = (f32[2048]{0:T(1024)}, f32[2048]{0:T(1024)S(1)}, u32[]{:S(2)}) copy-start(f32[2048]{0:T(1024)S(1)} %fusion.62) | copy-start | bytes 24580
  277.5 17.5 %copy-start.12 = (f32[2048]{0:T(1024)S(1)}, f32[2048]{0:T(1024)}, u32[]{:S(2)}) copy-start(f32[2048]{0:T(1024)} %copy-done.11) | copy-start | bytes 24580
  277.5 17.6 %copy-start.3 = (bf16[1,2048,1024]{1,2,0:T(8,128)(2,1)S(1)}, bf16[1,2048,1024]{1,2,0:T(8,128)(2,1)}, u32[]{:S(2)}) copy-start(bf16[1,2048,1024]{1,2,0:T(8,128)(2,1)} %copy.9) | copy-start | bytes 12582916
  277.5 17.6 %copy-start.4 = (bf16[2048,1024]{0,1:T(8,128)(2,1)S(1)}, bf16[2048,1024]{0,1:T(8,128)(2,1)}, u32[]{:S(2)}) copy-start(bf16[2048,1024]{0,1:T(8,128)(2,1)} %get-tuple-element.23) | copy-start | bytes 12582916
  298.6 2.0 copy-start.1
  316.5 148.2 %reduce-scatter.17.cloned.1.call-start = ((), (), s32[]{:S(2)}) async-start(), calls=%async_computation.11 | async-start | bytes 5898240 | tf_op jit(solution)/shard_map/reduce_scatter | solution.py:31
  338.6 126.1 %reduce-scatter.11.cloned.1.call-start = ((), (), s32[]{:S(2)}) async-start(), calls=%async_computation.8 | async-start | bytes 5898240 | tf_op jit(solution)/shard_map/reduce_scatter | solution.py:31
  338.7 31.8 %copy-start.8 = (f32[2048]{0:T(1024)S(1)}, f32[2048]{0:T(1024)}, u32[]{:S(2)}) copy-start(f32[2048]{0:T(1024)} %copy-done.7) | copy-start | bytes 24580
  370.5 20.3 %copy-start.10 = (f32[2048]{0:T(1024)S(1)}, f32[2048]{0:T(1024)}, u32[]{:S(2)}) copy-start(f32[2048]{0:T(1024)} %copy-done.9) | copy-start | bytes 24580
  390.8 78.0 %reduce-scatter.13.cloned.1.call-start = ((), (), s32[]{:S(2)}) async-start(), calls=%async_computation.9 | async-start | bytes 5898240 | tf_op jit(solution)/shard_map/reduce_scatter | solution.py:31
  411.2 96.8 %reduce-scatter.9.cloned.1.call-start = ((), (), s32[]{:S(2)}) async-start(), calls=%async_computation.7 | async-start | bytes 5898240 | tf_op jit(solution)/shard_map/reduce_scatter | solution.py:31
  427.8 119.2 %reduce-scatter.7.cloned.1.call-start = ((), (), s32[]{:S(2)}) async-start(), calls=%async_computation.6 | async-start | bytes 5898240 | tf_op jit(solution)/shard_map/reduce_scatter | solution.py:31
  444.5 190.4 %all-reduce.3.cloned.1.call-start = ((), (), s32[]{:S(2)}) async-start(), calls=%async_computation.18 | async-start | bytes 7864320 | tf_op jit(solution)/shard_map/psum | solution.py:31
  547.0 17.5 %copy-start.6 = (f32[2048]{0:T(1024)S(1)}, f32[2048]{0:T(1024)}, u32[]{:S(2)}) copy-start(f32[2048]{0:T(1024)} %copy-done.5) | copy-start | bytes 24580
  547.1 17.6 %copy-start = (bf16[1,2048,1024]{1,2,0:T(8,128)(2,1)S(1)}, bf16[1,2048,1024]{1,2,0:T(8,128)(2,1)}, u32[]{:S(2)}) copy-start(bf16[1,2048,1024]{1,2,0:T(8,128)(2,1)} %copy.10) | copy-start | bytes 12582916
  547.1 17.6 %copy-start.2 = (bf16[2048,1024]{0,1:T(8,128)(2,1)S(1)}, bf16[2048,1024]{0,1:T(8,128)(2,1)}, u32[]{:S(2)}) copy-start(bf16[2048,1024]{0,1:T(8,128)(2,1)} %copy-done.1) | copy-start | bytes 12582916
Sparse Core Ops, SparseCore 0:
  10.2 37.8 all-gather.12
  49.7 33.6 all-gather.14
  85.0 33.6 all-gather.16
  120.2 33.6 all-gather.20
  155.9 33.6 all-gather.22
  191.7 33.6 all-gather.18
  316.6 34.6 reduce-scatter.14
  353.6 36.8 reduce-scatter.16
  392.8 36.8 reduce-scatter.10
  431.9 36.8 reduce-scatter.12
  471.1 36.8 reduce-scatter.8
  510.1 36.8 reduce-scatter.6
  549.8 85.0 all-reduce.2
where the time goes:
time: 654 us; the launch traced here: 647 us
  matrix products  351 us (54%)
  waiting for transfers between devices  234 us (36%)
  local copies, waits for them, and re-layouts  30 us (5%)
  other arithmetic  17.2 us (3%)
  between operations  14.2 us (2%)
    dot_general x6, matrix products, layer(): up = jnp.dot(a, w['w_up'], preferred_element_type=jnp.float32)  128 us
    dot_general x6, matrix products, layer(): gate = jnp.dot(a, w['w_gate'], preferred_element_type=jnp.float32)  118 us
    dot_general x5, matrix products, matmul(): jnp.dot(a, w, preferred_element_type=jnp.float32).astype(jnp.bfloat16)  105 us
    all_gather x6, waiting for transfers between devices, fetched(): lax.all_gather(w[number], 's', axis=0, tiled=True)  90.9 us
    reduce_scatter x6, waiting for transfers between devices, summed(): lax.psum_scatter(term, 's', scatter_dimension=0, tiled=True)  82.2 us
    psum x1, waiting for transfers between devices, summed(): lax.psum(lax.psum_scatter(term, 's', scatter_dimension=0, tiled=True), 'r')  59.1 us
    unnamed x29, local copies, waits for them, and re-layouts  22.6 us
  transfers between devices with their start and end apart: 13, of which 10 were waited for; matrix products, arithmetic and copies ran while one was open for 46% of the time, Pallas kernels for 0%

commit v1 on v0

v1 whole, which is shorter than its diff:
```python
import jax
import jax.numpy as jnp
from jax import lax
from jax.experimental import pallas as pl
from jax.experimental.pallas import tpu as pltpu
from jax.sharding import PartitionSpec as P

bf16, f32 = jnp.bfloat16, jnp.float32
NT = (((1,), (1,)), ((), ()))
EPS = 1e-6
WIDE = 512
VMEM = 64 * 1024 * 1024 - 65536
def params(**more):
    return pltpu.CompilerParams(vmem_limit_bytes=VMEM, **more)


def whole(shape):
    return pl.BlockSpec(shape, lambda *i: (0,) * len(shape), pipeline_mode=pl.Buffered(1))


def cost(flops, nbytes):
    return pl.CostEstimate(flops=flops, bytes_accessed=nbytes, transcendentals=0)


def place():
    s = lax.axis_index("s")
    return s // 2, s % 2, lax.axis_index("r")


def solution(mesh):
    ns, nr = mesh.shape["s"], mesh.shape["r"]
    nx = ns // 2
    assert nx == 4 and nr == 4

    def owner(x, c, xr, other):
        return 2 * ((x + xr) % nx) + (c + other) % 2

    def neighbours():
        s, y = lax.axis_index("s"), lax.axis_index("r")
        return s, y, {
            "core": {"s": s + 1 - 2 * (s % 2)},
            "right": {"s": (s + 2) % ns},
            "left": {"s": (s + ns - 2) % ns},
            "up": {"r": (y + 1) % nr},
            "below": {"r": (y + nr - 1) % nr},
            "pair": {"r": y + 1 - 2 * (y % 2)},
            "cross": {"r": nr - 1 - y},
        }

    def greet(to, names):
        barrier = pltpu.get_barrier_semaphore()
        for name in names:
            pl.semaphore_signal(barrier, inc=1, device_id=to[name], device_id_type=pl.DeviceIdType.MESH)
        pl.semaphore_wait(barrier, len(names))

    def remote(src, dst, send, recv, device):
        return pltpu.make_async_remote_copy(src_ref=src, dst_ref=dst, send_sem=send, recv_sem=recv, device_id=device, device_id_type=pl.DeviceIdType.MESH)

    class Summing:
        def __init__(self, mine, chunks):
            _, self.rows, self.n = mine.shape
            self.k, self.h = chunks, self.rows // chunks
            assert self.rows % chunks == 0 and self.h % 32 == 0
            self.last = chunks + 3
            whole_, halves, block = (nx, self.rows, self.n), (chunks, 2, self.h // 2, self.n), (chunks, self.h, self.n)
            self.in_specs = [pl.BlockSpec(memory_space=pl.ANY)] * 2
            self.out_spec = pl.BlockSpec((self.rows, self.n), lambda *i: (0, 0), pipeline_mode=pl.Buffered(1))
            self.out_shape = jax.ShapeDtypeStruct((self.rows, self.n), bf16)
            self.scratch = [pltpu.VMEM(s, bf16) for s in (whole_,) * 3 + (halves,) * 4 + (block,) * 4]
            self.scratch += [pltpu.SemaphoreType.DMA((chunks,)), pltpu.SemaphoreType.DMA((9, chunks)), pltpu.SemaphoreType.DMA((9, chunks))]

        def bind(self, mine, theirs, out, scratch):
            self.mine, self.theirs, self.out = mine, theirs, out
            self.own, self.other, self.t, self.far, self.near, self.acc, self.got, self.b1, self.y1, self.b2, self.y2, self.load_sem, self.send, self.recv = scratch
            _, _, self.to = neighbours()

        def part(self, k, half=None):
            if half is None:
                return pl.ds(pl.multiple_of(k * self.h, 32), self.h)
            return pl.ds(pl.multiple_of(k * self.h + half * (self.h // 2), 16), self.h // 2)

        def load(self, k):
            return pltpu.make_async_copy(self.mine.at[:, self.part(k)], self.own.at[:, self.part(k)], self.load_sem.at[k])

        def copy(self, which, k):
            src, dst, to = (
                lambda: (self.theirs.at[:, self.part(k)], self.other.at[:, self.part(k)], "core"),
                lambda: (self.t.at[2, self.part(k, 0)], self.far.at[k, 0], "left"),
                lambda: (self.t.at[2, self.part(k, 1)], self.far.at[k, 1], "right"),
                lambda: (self.t.at[1, self.part(k, 0)], self.near.at[k, 0], "right"),
                lambda: (self.t.at[3, self.part(k, 1)], self.near.at[k, 1], "left"),
                lambda: (self.acc.at[k, 0], self.got.at[k, 0], "left"),
                lambda: (self.acc.at[k, 1], self.got.at[k, 1], "right"),
                lambda: (self.b1.at[k], self.y1.at[k], "pair"),
                lambda: (self.b2.at[k], self.y2.at[k], "cross"),
            )[which]()
            return remote(src, dst, self.send.at[which, k], self.recv.at[which, k], self.to[to])

        def start(self):
            greet(self.to, ("core", "right", "left", "pair", "cross"))

            def go(k, _):
                self.copy(0, k).start()
                self.load(k).start()
                return 0

            lax.fori_loop(0, self.k, go, 0)

        def step(self, i):
            wide = lambda v: v.astype(f32)

            def when(k, f):
                if isinstance(k, int):
                    if 0 <= k < self.k:
                        f(k)
                else:
                    pl.when((k >= 0) & (k < self.k))(lambda: f(k))

            def cores(k):
                self.load(k).wait()
                self.copy(0, k).wait_recv()
                for p in (2, 1, 3, 0):
                    self.t[p, self.part(k)] = (wide(self.own[p, self.part(k)]) + wide(self.other[p, self.part(k)])).astype(bf16)
                for which in (1, 2, 3, 4):
                    self.copy(which, k).start()

            def far(k):
                for half, p in ((0, 3), (1, 1)):
                    self.copy(1 + half, k).wait_recv()
                    self.acc[k, half] = (wide(self.t[p, self.part(k, half)]) + wide(self.far[k, half])).astype(bf16)
                    self.copy(5 + half, k).start()

            def block(k):
                for half in (0, 1):
                    self.copy(3 + half, k).wait_recv()
                    self.copy(5 + half, k).wait_recv()
                    total = wide(self.t[0, self.part(k, half)]) + wide(self.near[k, half]) + wide(self.got[k, half])
                    self.b1[k, pl.ds(half * (self.h // 2), self.h // 2)] = total.astype(bf16)
                self.copy(7, k).start()

            def pair(k):
                self.copy(7, k).wait_recv()
                self.b2[k] = (wide(self.b1[k]) + wide(self.y1[k])).astype(bf16)
                self.copy(8, k).start()

            def cross(k):
                self.copy(8, k).wait_recv()
                self.out[self.part(k), :] = (wide(self.b2[k]) + wide(self.y2[k])).astype(bf16)

            for back, f in enumerate((cores, far, block, pair, cross)):
                when(i - back, f)

        def finish(self):
            def sent(k, _):
                for which in range(9):
                    self.copy(which, k).wait_send()
                return 0

            lax.fori_loop(0, self.k, sent, 0)

    def fetched(gate, up):
        rows, ff = gate.shape
        n = rows // nr
        count = 48

        def kernel(g_ref, u_ref, out, buf, local, send, recv):
            s, y, to = neighbours()
            o = {"L": (s + ns - 2) % ns, "R": (s + 2) % ns, "F": (s + ns // 2) % ns}
            q = {0: y, -1: (y + nr - 1) % nr, 1: (y + 1) % nr, 2: (y + 2) % nr}
            used = []

            def put(src, dst, name):
                i = len(used)
                c = remote(src, dst, send.at[i], recv.at[i], to[name])
                c.start()
                used.append(c)
                return c

            def pass_on(ref, name):
                return put(ref, ref, name)

            greet(to, ("core", "right", "left", "up", "below"))
            loads = [pltpu.make_async_copy(r, buf.at[m], local.at[m]) for m, r in enumerate((g_ref, u_ref))]
            for c in loads:
                c.start()
            mine = pl.multiple_of(y * n, 16)

            def rows_of(who, share, half=None):
                first, many = (0, n) if half is None else (half * (n // 2), n // 2)
                return out.at[o[who], 1, pl.ds(pl.multiple_of(q[share] * n + first, 16), many)]

            src = u_ref.at[pl.ds(mine, n)]
            dst = out.at[s, 1, pl.ds(mine, n)]
            from_left, from_right = put(src, dst, "right"), put(src, dst, "left")
            a_left, a_right = put(g_ref, out.at[s, 0], "right"), put(g_ref, out.at[s, 0], "left")
            cores = [put(g_ref, out.at[s, 0], "core"), put(u_ref, out.at[s, 1], "core")]
            up_from, below_from = {}, {}
            late = []
            for c, who, half in ((from_left, "L", None), (from_right, "R", None), (None, "F", 0), (None, "F", 1)):
                if half is not None:
                    c = fars[half]
                c.wait_recv()
                if who == "L":
                    fars = [pass_on(rows_of("L", 0, 0), "right"), None]
                elif who == "R":
                    fars[1] = pass_on(rows_of("R", 0, 1), "left")
                ref = rows_of(who, 0, half)
                below_from[who, half] = pass_on(ref, "up")
                up_from[who, half] = pass_on(ref, "below")
                cores.append(pass_on(ref, "core"))
            half = rows // 2
            a_left.wait_recv()
            far_upper = pass_on(out.at[o["L"], 0, pl.ds(0, half)], "right")
            cores.append(pass_on(out.at[o["L"], 0], "core"))
            a_right.wait_recv()
            far_lower = pass_on(out.at[o["R"], 0, pl.ds(half, half)], "left")
            cores.append(pass_on(out.at[o["R"], 0], "core"))
            for c in loads:
                c.wait()
            store = pltpu.make_async_copy(buf, out.at[s], local.at[2])
            store.start()
            for who, part in (("L", None), ("R", None), ("F", 0), ("F", 1)):
                below_from[who, part].wait_recv()
                ref = rows_of(who, -1, part)
                if (who, part) in (("L", None), ("F", 0)):
                    late.append((pass_on(ref, "up"), rows_of(who, 2, part)))
                cores.append(pass_on(ref, "core"))
                up_from[who, part].wait_recv()
                ref = rows_of(who, 1, part)
                if (who, part) in (("R", None), ("F", 1)):
                    late.append((pass_on(ref, "below"), rows_of(who, 2, part)))
                cores.append(pass_on(ref, "core"))
            for c, ref in late:
                c.wait_recv()
                cores.append(pass_on(ref, "core"))
            far_upper.wait_recv()
            cores.append(pass_on(out.at[o["F"], 0, pl.ds(0, half)], "core"))
            far_lower.wait_recv()
            cores.append(pass_on(out.at[o["F"], 0, pl.ds(half, half)], "core"))
            for c in cores:
                c.wait_recv()
            for c in used:
                c.wait_send()
            store.wait()
            assert len(used) <= count

        anywhere = pl.BlockSpec(memory_space=pl.ANY)
        return pl.pallas_call(
            kernel,
            name="fetched",
            in_specs=[anywhere] * 2,
            out_specs=anywhere,
            out_shape=jax.ShapeDtypeStruct((ns, 2, rows, ff), bf16),
            scratch_shapes=[pltpu.VMEM((2, rows, ff), bf16), pltpu.SemaphoreType.DMA((3,)), pltpu.SemaphoreType.DMA((count,)), pltpu.SemaphoreType.DMA((count,))],
            compiler_params=params(collective_id=0, has_side_effects=True),
            cost_estimate=cost(20 * 1000 * 1000 * 1000, 4 * ns * rows * ff),
        )(gate, up)

    def gate_up(h, pair):
        t, d = h.shape
        ff = pair.shape[-1]
        r = 512
        steps = t // r
        share = d // ns
        groups = [(0, WIDE), (WIDE, ff)]

        def kernel(h_ref, pair_ref, s1, s2, act_o, actt_o, at_o, w_s, a_s, sem):
            i = pl.program_id(0)

            def load(m, k):
                lo, hi = groups[k]
                return pltpu.make_async_copy(pair_ref.at[:, m, :, pl.ds(lo, hi - lo)], w_s.at[m, :, :, pl.ds(lo, hi - lo)], sem.at[m, k])

            @pl.when(i == 0)
            def _():
                for k in range(len(groups)):
                    for m in range(2):
                        load(m, k).start()

            w = h_ref[...].astype(f32)
            a_s[...] = (w * lax.rsqrt(jnp.mean(w * w, -1, keepdims=True) + EPS)).astype(bf16)
            x, c, _ = place()
            for p in range(ns):
                s = owner(x, c, p % nx, p // nx)
                at_o[p * share : (p + 1) * share, :] = a_s[:, pl.ds(pl.multiple_of(s * share, share), share)].T
            for k in range(0, ff, WIDE):
                if k <= WIDE:
                    @pl.when(i == 0)
                    def _(k=k):
                        for m in range(2):
                            load(m, k // WIDE).wait()
                cols = slice(k, k + WIDE)
                a = a_s[...]
                g, u = (jnp.dot(a, w_s[m, :, :, cols].reshape(d, WIDE), preferred_element_type=f32) for m in range(2))
                sg = jax.nn.sigmoid(g)
                silu = g * sg
                s1[:, cols] = silu
                s2[:, cols] = u * (sg + silu * (1 - sg))
                act = (silu * u).astype(bf16)
                act_o[:, cols] = act
                actt_o[cols, :] = act.T

        rows = lambda n: pl.BlockSpec((r, n), lambda i: (i, 0))
        cols = lambda n: pl.BlockSpec((n, r), lambda i: (0, i))
        shape = jax.ShapeDtypeStruct
        return pl.pallas_call(
            kernel,
            grid=(steps,),
            name="gate_up",
            in_specs=[rows(d), pl.BlockSpec(memory_space=pl.ANY)],
            out_specs=[rows(ff), rows(ff), rows(ff), cols(ff), cols(d)],
            out_shape=[shape((t, ff), f32), shape((t, ff), f32), shape((t, ff), bf16), shape((ff, t), bf16), shape((d, t), bf16)],
            scratch_shapes=[pltpu.VMEM((2, ns, share, ff), bf16), pltpu.VMEM((r, d), bf16), pltpu.SemaphoreType.DMA((2, 2))],
            compiler_params=params(),
            cost_estimate=cost(4 * t * d * ff, 14 * t * ff),
        )(h, pair)

    def down(h, act, w):
        t, d = h.shape
        ff = act.shape[1]
        r = 512

        def kernel(h_ref, act_ref, w_ref, o_ref):
            y = jnp.dot(act_ref[...], w_ref[...], preferred_element_type=f32).astype(bf16)
            o_ref[...] = (h_ref[...].astype(f32) + y.astype(f32)).astype(bf16)

        rows = lambda n: pl.BlockSpec((r, n), lambda i: (i, 0))
        return pl.pallas_call(
            kernel,
            grid=(t // r,),
            name="down",
            in_specs=[rows(d), rows(ff), whole((ff, d))],
            out_specs=rows(d),
            out_shape=jax.ShapeDtypeStruct((t, d), bf16),
            compiler_params=params(),
            cost_estimate=cost(2 * t * d * ff, 2 * t * ff),
        )(h, act, w)

    def by_down(actt, dy, split):
        ff, t = actt.shape
        d = dy.shape[1]
        pair = ff // nx
        share = pair // 2

        def kernel(pos, actt_ref, dy_ref, *out):
            w = jnp.dot(actt_ref[...], dy_ref[...], preferred_element_type=f32).astype(bf16)
            if not split:
                out[0][...] = w
                return
            mine, theirs = out
            c = lax.axis_index("s") % 2

            @pl.when(c == 0)
            def _():
                mine[0], theirs[0] = w[:share], w[share:]

            @pl.when(c == 1)
            def _():
                mine[0], theirs[0] = w[share:], w[:share]

        block = pl.BlockSpec((1, share, d), lambda i, pos: (i, 0, 0))
        first = (lax.axis_index("s") // 2 if split else jnp.int32(0)).astype(jnp.int32)
        return pl.pallas_call(
            kernel,
            name="by_down",
            grid_spec=pltpu.PrefetchScalarGridSpec(
                num_scalar_prefetch=1,
                grid=(nx,),
                in_specs=[pl.BlockSpec((pair, t), lambda i, pos: ((pos[0] + i) % nx, 0)), pl.BlockSpec((t, d), lambda i, pos: (0, 0), pipeline_mode=pl.Buffered(1))],
                out_specs=[block, block] if split else pl.BlockSpec((pair, d), lambda i, pos: (i, 0)),
            ),
            out_shape=[jax.ShapeDtypeStruct((nx, share, d), bf16)] * 2 if split else jax.ShapeDtypeStruct((ff, d), bf16),
            compiler_params=params(),
            cost_estimate=cost(2 * t * d * ff, 2 * t * ff),
        )(first[None], actt, dy)

    def by_gate_up(dy, at, w, s1, s2, terms=None):
        t, d = dy.shape
        share = d // ns
        ff = s1.shape[1]
        r = 512
        work = Summing(terms[0], 5) if terms else None

        def kernel(*refs):
            if work:
                dy_ref, at_hbm, w_ref, s1_ref, s2_ref, m_ref, t_ref, dg, du, mine, theirs, out, at_ref, sem, *scratch = refs
                work.bind(m_ref, t_ref, out, scratch)
            else:
                dy_ref, at_hbm, w_ref, s1_ref, s2_ref, dg, du, plain, at_ref, sem = refs
            x, c, _ = place()
            load = pltpu.make_async_copy(at_hbm, at_ref, sem)
            j = pl.program_id(0)

            @pl.when(j == 0)
            def _():
                load.start()
                if work:
                    work.start()

            for k in range(0, t, r):
                rows = slice(k, k + r)
                back = lax.dot_general(dy_ref[rows, :], w_ref[...], NT, preferred_element_type=f32).astype(bf16).astype(f32)
                dg[rows, :] = (back * s2_ref[rows, :]).astype(bf16)
                du[rows, :] = (back * s1_ref[rows, :]).astype(bf16)

            @pl.when(j == 0)
            def _():
                load.wait()

            for k, ref in enumerate((dg, du)):
                if work:
                    work.step(2 * j + k)
                term = jnp.dot(at_ref[...], ref[...], preferred_element_type=f32).astype(bf16)
                to = slice(k * share, (k + 1) * share)
                for p in range(ns):
                    block = term[p * share : (p + 1) * share]
                    if not work:
                        plain[owner(x, c, p % nx, p // nx), to] = block
                    elif p < nx:
                        mine[p, to] = block
                    else:
                        theirs[p - nx, to] = block

            if work:
                assert work.last < 2 * (ff // WIDE)

                @pl.when(j == ff // WIDE - 1)
                def _():
                    work.finish()

        cols = lambda n: pl.BlockSpec((n, WIDE), lambda j: (0, j))
        many, parts = (2, nx) if work else (1, ns)
        block = pl.BlockSpec((parts, 2 * share, WIDE), lambda j: (0, 0, j))
        shape = jax.ShapeDtypeStruct
        return pl.pallas_call(
            kernel,
            grid=(ff // WIDE,),
            name="by_gate_up",
            in_specs=[whole((t, d)), pl.BlockSpec(memory_space=pl.ANY), pl.BlockSpec((WIDE, d), lambda j: (j, 0)), cols(t), cols(t)] + (work.in_specs if work else []),
            out_specs=[cols(t), cols(t)] + [block] * many + ([work.out_spec] if work else []),
            out_shape=[shape((t, ff), bf16)] * 2 + [shape((parts, 2 * share, ff), bf16)] * many + ([work.out_shape] if work else []),
            scratch_shapes=[pltpu.VMEM((d, t), bf16), pltpu.SemaphoreType.DMA(())] + (work.scratch if work else []),
            compiler_params=params(collective_id=1, has_side_effects=True) if work else params(),
            cost_estimate=cost(6 * t * d * ff, 12 * t * ff),
        )(dy, at, w, s1, s2, *(terms or ()))

    def by_input(dg, du, pair, h, dy, terms=None):
        t, d = h.shape
        ff = dg.shape[1]
        share = d // ns
        r = 256
        steps = t // r
        work = Summing(terms[0], 8) if terms else None

        def kernel(*refs):
            if work:
                dg_ref, du_ref, wg_ref, wu_ref, h_ref, dy_ref, m_ref, t_ref, o_ref, out, *scratch = refs
                work.bind(m_ref, t_ref, out, scratch)

                @pl.when(pl.program_id(0) == 0)
                def _():
                    work.start()
            else:
                dg_ref, du_ref, wg_ref, wu_ref, h_ref, dy_ref, o_ref = refs
            da = sum(
                lax.dot_general(x[...], w[...].reshape(d, ff), NT, preferred_element_type=f32) for x, w in ((dg_ref, wg_ref), (du_ref, wu_ref))
            )
            wide = h_ref[...].astype(f32)
            scale = lax.rsqrt(jnp.mean(wide * wide, -1, keepdims=True) + EPS)
            back = scale * (da - wide * (scale * scale * jnp.mean(da * wide, -1, keepdims=True)))
            o_ref[...] = (dy_ref[...].astype(f32) + back).astype(bf16)
            if work:
                work.step(pl.program_id(0))

                @pl.when(pl.program_id(0) == steps - 1)
                def _():
                    def rest(i, _):
                        work.step(i)
                        return 0

                    lax.fori_loop(steps, work.last + 1, rest, 0)
                    work.finish()

        rows = lambda n: pl.BlockSpec((r, n), lambda i: (i, 0))
        matrix = lambda m: pl.BlockSpec((ns, None, share, ff), lambda i: (0, m, 0, 0), pipeline_mode=pl.Buffered(1))
        shape = jax.ShapeDtypeStruct((t, d), bf16)
        return pl.pallas_call(
            kernel,
            grid=(steps,),
            name="by_input",
            in_specs=[rows(ff)] * 2 + [matrix(0), matrix(1)] + [rows(d)] * 2 + (work.in_specs if work else []),
            out_specs=[rows(d), work.out_spec] if work else rows(d),
            out_shape=[shape, work.out_shape] if work else shape,
            scratch_shapes=work.scratch if work else [],
            compiler_params=params(collective_id=2, has_side_effects=True) if work else params(),
            cost_estimate=cost(4 * t * d * ff, 4 * t * ff),
        )(dg, du, pair, pair, h, dy, *(terms or ()))

    def step(x, dy, *weights):
        layers, share, _ = weights[0].shape
        h, dy = x[0], dy[0]
        summed = lambda term: lax.psum(lax.psum_scatter(term, "s", scatter_dimension=0, tiled=True), "r")
        whole_of = lambda w: lax.all_gather(w, "s", axis=0, tiled=True)

        kept = []
        for number in range(layers):
            gate, up = weights[0][number], weights[1][number]
            if number == 0:
                pair = fetched(gate, up)
            else:
                pair = whole_of(jnp.concatenate([gate, up])).reshape(ns, 2, share, -1)
            wd = whole_of(weights[2][number])
            s1, s2, act, actt, at = gate_up(h, pair)
            kept.append((h, s1, s2, actt, at, pair, wd))
            if number < layers - 1:
                h = down(h, act, wd)
        grads = [None] * layers
        for number in reversed(range(layers)):
            h, s1, s2, actt, at, pair, wd = kept[number]
            down_terms = by_down(actt, dy, number == 0)
            if number == 0:
                dg, du, *terms, g_down = by_gate_up(dy, at, wd, s1, s2, down_terms)
                dy, g_pair = by_input(dg, du, pair, h, dy, terms)
            else:
                dg, du, terms = by_gate_up(dy, at, wd, s1, s2)
                dy = by_input(dg, du, pair, h, dy)
                g_down, g_pair = (summed(v) for v in (down_terms, terms.reshape(2 * share * ns, -1)))
            grads[number] = (g_pair[:share], g_pair[share:], g_down)
        return (dy[None], *(jnp.stack([g[i] for g in grads]) for i in range(3)))

    states, cut = P(("rep", "r", "s"), None, None), P(None, "s", None)
    return jax.shard_map(
        step,
        mesh=mesh,
        in_specs=(states, states) + (cut,) * 3,
        out_specs=(states,) + (P("rep", "s", None),) * 3,
        check_vma=False,
    )
```

time: 654 us -> 438 us (0.67)
  Pallas kernels: 0 us -> 400 us
  matrix products: 351 us -> 0 us
  waiting for transfers between devices: 234 us -> 1.09 us
  local copies, waits for them, and re-layouts: 30 us -> 9.6 us
  other arithmetic: 17.2 us -> 4.65 us
    pallas_call x0 -> x10, Pallas kernels: none -> 400 us  [the longest x2 112 us: by_input(): pl.pallas_call(kernel, grid=(steps,), name='by_input', in_specs=[rows(ff)...]
    dot_general x17 -> x0, matrix products: 351 us -> none  [the longest x6 128 us: layer(): up = jnp.dot(a, w['w_up'], preferred_element_type=jnp.float32)]
    all_gather x6 -> x3, waiting for transfers between devices: 90.9 us -> 0.04 us  [step(): whole_of = lambda w: lax.all_gather(w, 's', axis=0, tiled=True)]
    reduce_scatter x6 -> x2, waiting for transfers between devices: 82.2 us -> 0.04 us  [step(): lax.psum_scatter(term, 's', scatter_dimension=0, tiled=True)]
    psum x1, waiting for transfers between devices: 59.1 us -> 0.02 us  [step(): lax.psum(lax.psum_scatter(term, 's', scatter_dimension=0, tiled=True), 'r')]
    unnamed x29 -> x11, local copies, waits for them, and re-layouts: 22.6 us -> 2.84 us
  transfers between devices with their start and end apart: 13 -> 6, of which waited for: 10 -> 0; matrix products, arithmetic and copies ran while one was open for 46% -> 1% of each run, Pallas kernels for 0% -> 93%
where the time goes in v1:
time: 438 us; the launch traced here: 430 us
  Pallas kernels  400 us (91%)
  between operations  14.7 us (3%)
  local copies, waits for them, and re-layouts  9.6 us (2%)
  other arithmetic  4.65 us (1%)
    pallas_call x2, Pallas kernels, by_input(): pl.pallas_call(kernel, grid=(steps,), name='by_input', in_specs=[rows(ff)...  112 us
    pallas_call x2, Pallas kernels, by_gate_up(): pl.pallas_call(kernel, grid=(ff // WIDE,), name='by_gate_up', in_specs=[w...  105 us
    pallas_call x2, Pallas kernels, gate_up(): pl.pallas_call(kernel, grid=(steps,), name='gate_up', in_specs=[rows(d),...  75 us
    pallas_call x1, Pallas kernels, fetched(): pl.pallas_call(kernel, name='fetched', in_specs=[anywhere] * 2, out_specs...  59.7 us
    pallas_call x2, Pallas kernels, by_down(): pl.pallas_call(kernel, name='by_down', grid_spec=pltpu.PrefetchScalarGrid...  31.8 us
    pallas_call x1, Pallas kernels, down(): pl.pallas_call(kernel, grid=(t // r,), name='down', in_specs=[rows(d), ro...  16.3 us
  transfers between devices with their start and end apart: 6, of which 0 were waited for; matrix products, arithmetic and copies ran while one was open for 1% of the time, Pallas kernels for 93%

profile of v1, /device:TPU:97, one launch (start us, length us, event | category | flops | bytes accessed | tf_op | source)
XLA Modules:
  0.0 430.1 jit_solution(14750795047306565291)
XLA Ops:
  7.2 0.1 all-gather.8.cloned.1.call-start
  7.3 2.6 fusion
  9.9 0.1 all-gather.8.cloned.1.call-update
  9.9 0.1 all-gather.6.cloned.1.call-start
  10.0 1.3 slice_bitcast_fusion.4
  11.3 1.1 pad_maximum_fusion
  12.4 0.1 all-gather.6.cloned.1.call-update
  12.5 0.1 all-gather.10.cloned.1.call-start
  12.6 0.7 all-gather.10.cloned.1.call-update
  13.3 0.1 reduce-scatter.5.cloned.1.call-start
  13.4 59.7 %fetched.1.pair_ref.refs_2_.refs_3_ = bf16[8,2,128,2560]{3,2,1,0:T(8,128)(2,1)} custom-call(bf16[128,2560]{1,0:T(8,128)(2,1)} %get-tuple-element.58.g_ref, bf16[128,2560]{1,0:T(8,128)(2,1)} %get-tuple-element.57.u_ref), custom_call_target="tpu_custom_call" | custom-call | flops 20000000000 | bytes 10485760 | tf_op jit(solution)/shard_map/fetched/pallas_call | solution.py:248
  73.1 37.4 %gate_up.2 = (f32[2048,2560]{1,0:T(8,128)}, f32[2048,2560]{1,0:T(8,128)}, bf16[2048,2560]{1,0:T(8,128)(2,1)}, bf16[2560,2048]{1,0:T(8,128)(2,1)}, bf16[1024,2048]{1,0:T(8,128)(2,1)}) custom-call(bf16[2048,1024]{1,0:T(8,128)(2,1)} %bitcast.39, bf16[8,2,128,2560]{3,2,1,0:T(8,128)(2,1)} %fetched.1.pair_ref.refs_2_.refs_3_), custom_call_target="tpu_custom_call" | custom-call | flops 21474836480 | bytes 73400320 | tf_op jit(solution)/shard_map/gate_up/pallas_call | solution.py:306
  110.5 16.3 %down.1.h_ref.refs_4_ = bf16[2048,1024]{1,0:T(8,128)(2,1)} custom-call(bf16[2048,1024]{1,0:T(8,128)(2,1)} %bitcast.40, bf16[2048,2560]{1,0:T(8,128)(2,1)} %get-tuple-element.25.act_ref, bf16[2560,1024]{1,0:T(8,128)(2,1)} %bitcast.33), custom_call_target="tpu_custom_call" | custom-call | flops 10737418240 | bytes 10485760 | tf_op jit(solution)/shard_map/down/pallas_call | solution.py:328
  126.8 37.6 %gate_up.3 = (f32[2048,2560]{1,0:T(8,128)}, f32[2048,2560]{1,0:T(8,128)}, bf16[2048,2560]{1,0:T(8,128)(2,1)}, bf16[2560,2048]{1,0:T(8,128)(2,1)}, bf16[1024,2048]{1,0:T(8,128)(2,1)}) custom-call(bf16[2048,1024]{1,0:T(8,128)(2,1)} %down.1.h_ref.refs_4_, bf16[8,2,128,2560]{3,2,1,0:T(8,128)(2,1)} %bitcast.30), custom_call_target="tpu_custom_call" | custom-call | flops 21474836480 | bytes 73400320 | tf_op jit(solution)/shard_map/gate_up/pallas_call | solution.py:306
  164.4 15.7 %by_down.3 = bf16[2560,1024]{1,0:T(8,128)(2,1)} custom-call(s32[1]{0:T(128)} %constant.19.clone.1.pos, bf16[2560,2048]{1,0:T(8,128)(2,1)} %get-tuple-element.45.actt_ref, bf16[2048,1024]{1,0:T(8,128)(2,1)} %bitcast.36), custom_call_target="tpu_custom_call" | custom-call | flops 10737418240 | bytes 10485760 | tf_op jit(solution)/shard_map/by_down/pallas_call | solution.py:363
  180.0 0.1 reduce-scatter.5.cloned.1.call-update
  180.1 0.1 reduce-scatter.3.cloned.1.call-start
  180.2 46.5 %by_gate_up.2 = (bf16[2048,2560]{1,0:T(8,128)(2,1)}, bf16[2048,2560]{1,0:T(8,128)(2,1)}, bf16[8,256,2560]{2,1,0:T(8,128)(2,1)}) custom-call(bf16[2048,1024]{1,0:T(8,128)(2,1)} %bitcast.37, bf16[1024,2048]{1,0:T(8,128)(2,1)} %get-tuple-element.26.refs_1_, bf16[2560,1024]{1,0:T(8,128)(2,1)} %bitcast.35, f32[2048,2560]{1,0:T(8,128)} %get-tuple-element.27.refs_3_, ...), custom_call_target="tpu_custom_call" | custom-call | flops 32212254720 | bytes 62914560 | tf_op jit(solution)/shard_map/by_gate_up/pallas_call | solution.py:435
  226.7 0.1 reduce-scatter.3.cloned.1.call-update
  226.8 0.1 all-reduce.3.cloned.1.call-start
  226.9 31.5 %by_input.2.dy_ref.refs_0_.refs_5_ = bf16[2048,1024]{1,0:T(8,128)(2,1)} custom-call(bf16[2048,2560]{1,0:T(8,128)(2,1)} %get-tuple-element.29.refs_0_, bf16[2048,2560]{1,0:T(8,128)(2,1)} %get-tuple-element.30.refs_1_, bf16[8,2,128,2560]{3,2,1,0:T(8,128)(2,1)} %bitcast.31, bf16[8,2,128,2560]{3,2,1,0:T(8,128)(2,1)} %bitcast.32, ...), custom_call_target="tpu_custom_call" | custom-call | flops 21474836480 | bytes 20971520 | tf_op jit(solution)/shard_map/by_input/pallas_call | solution.py:487
  258.3 16.2 %by_down.2 = (bf16[4,320,1024]{2,1,0:T(8,128)(2,1)}, bf16[4,320,1024]{2,1,0:T(8,128)(2,1)}) custom-call(s32[1]{0:T(128)} %bitcast.9.pos, bf16[2560,2048]{1,0:T(8,128)(2,1)} %get-tuple-element.34.actt_ref, bf16[2048,1024]{1,0:T(8,128)(2,1)} %by_input.2.dy_ref.refs_0_.refs_5_), custom_call_target="tpu_custom_call" | custom-call | flops 10737418240 | bytes 10485760 | tf_op jit(solution)/shard_map/by_down/pallas_call | solution.py:363
  274.5 58.6 %by_gate_up.3 = (bf16[2048,2560]{1,0:T(8,128)(2,1)}, bf16[2048,2560]{1,0:T(8,128)(2,1)}, bf16[4,256,2560]{2,1,0:T(8,128)(2,1)}, bf16[4,256,2560]{2,1,0:T(8,128)(2,1)}, bf16[320,1024]{1,0:T(8,128)(2,1)}) custom-call(bf16[2048,1024]{1,0:T(8,128)(2,1)} %by_input.2.dy_ref.refs_0_.refs_5_, bf16[1024,2048]{1,0:T(8,128)(2,1)} %get-tuple-element.31.refs_1_, ...), custom_call_target="tpu_custom_call" | custom-call | flops 32212254720 | bytes 62914560 | tf_op jit(solution)/shard_map/by_gate_up/pallas_call | solution.py:435
  333.2 0.1 all-reduce.3.cloned.1.call-update
  333.2 80.3 %by_input.3 = (bf16[2048,1024]{1,0:T(8,128)(2,1)}, bf16[256,2560]{1,0:T(8,128)(2,1)}) custom-call(bf16[2048,2560]{1,0:T(8,128)(2,1)} %get-tuple-element.37.refs_0_, bf16[2048,2560]{1,0:T(8,128)(2,1)} %get-tuple-element.38.refs_1_, bf16[8,2,128,2560]{3,2,1,0:T(8,128)(2,1)} %fetched.1.pair_ref.refs_2_.refs_3_, ...), custom_call_target="tpu_custom_call" | custom-call | flops 21474836480 | bytes 20971520 | tf_op jit(solution)/shard_map/by_input/pallas_call | solution.py:487
  413.5 1.4 slice_bitcast_fusion.2
  415.0 1.4 slice_bitcast_fusion
  416.5 1.2 pad_maximum_fusion.3
  417.6 1.2 pad_maximum_fusion.2
  418.8 1.2 pad_maximum_fusion.1
  420.0 0.8 copy-done
  420.8 2.0 copy.12
  (15 shorter events, 0.1 us)
Async XLA Ops:
  7.2 2.8 copy-start.2
  7.2 2.8 copy-start.1
  7.2 103.3 %all-gather.8.cloned.1.call-start = ((), (), s32[]{:S(2)}) async-start(), calls=%async_computation.5 | async-start | bytes 5898240 | tf_op jit(solution)/shard_map/all_gather | solution.py:503
  9.9 116.9 %all-gather.6.cloned.1.call-start = ((), (), s32[]{:S(2)}) async-start(), calls=%async_computation.2 | async-start | bytes 11796480 | tf_op jit(solution)/shard_map/all_gather | solution.py:503
  12.5 167.7 %all-gather.10.cloned.1.call-start = ((), (), s32[]{:S(2)}) async-start(), calls=%async_computation.6 | async-start | bytes 5898240 | tf_op jit(solution)/shard_map/all_gather | solution.py:503
  13.3 319.8 %reduce-scatter.5.cloned.1.call-start = ((), (), s32[]{:S(2)}) async-start(), calls=%async_computation.4 | async-start | bytes 5898240 | tf_op jit(solution)/shard_map/reduce_scatter | solution.py:502
  180.1 153.1 %reduce-scatter.3.cloned.1.call-start = ((), (), s32[]{:S(2)}) async-start(), calls=%async_computation.3 | async-start | bytes 11796480 | tf_op jit(solution)/shard_map/reduce_scatter | solution.py:502
  226.8 188.2 %all-reduce.3.cloned.1.call-start = ((), (), s32[]{:S(2)}) async-start(), calls=%async_computation.7 | async-start | bytes 3932160 | tf_op jit(solution)/shard_map/psum | solution.py:502
  413.5 2.9 copy-start.3
  415.0 1.5 copy-start.4
  417.6 3.1 copy-start
Sparse Core Ops, SparseCore 0:
  10.1 58.1 all-gather.7
  70.4 55.5 all-gather.5
  127.6 33.8 all-gather.9
  180.2 34.0 reduce-scatter.4
  226.9 58.5 reduce-scatter.2
  333.4 69.2 all-reduce.2

commit v2 on v1

--- a/solution.py
+++ b/solution.py
@@ -9,7 +9,10 @@
 NT = (((1,), (1,)), ((), ()))
 EPS = 1e-6
 WIDE = 512
+FIRST = 3
 VMEM = 64 * 1024 * 1024 - 65536
+
+
 def params(**more):
     return pltpu.CompilerParams(vmem_limit_bytes=VMEM, **more)
 
@@ -161,7 +164,7 @@
     def fetched(gate, up):
         rows, ff = gate.shape
         n = rows // nr
-        count = 48
+        count = 80
 
         def kernel(g_ref, u_ref, out, buf, local, send, recv):
             s, y, to = neighbours()
@@ -185,58 +188,46 @@
                 c.start()
             mine = pl.multiple_of(y * n, 16)
 
-            def rows_of(who, share, half=None):
+            def rows_of(m, who, share, half=None):
                 first, many = (0, n) if half is None else (half * (n // 2), n // 2)
-                return out.at[o[who], 1, pl.ds(pl.multiple_of(q[share] * n + first, 16), many)]
-
-            src = u_ref.at[pl.ds(mine, n)]
-            dst = out.at[s, 1, pl.ds(mine, n)]
-            from_left, from_right = put(src, dst, "right"), put(src, dst, "left")
-            a_left, a_right = put(g_ref, out.at[s, 0], "right"), put(g_ref, out.at[s, 0], "left")
-            cores = [put(g_ref, out.at[s, 0], "core"), put(u_ref, out.at[s, 1], "core")]
-            up_from, below_from = {}, {}
-            late = []
-            for c, who, half in ((from_left, "L", None), (from_right, "R", None), (None, "F", 0), (None, "F", 1)):
-                if half is not None:
-                    c = fars[half]
-                c.wait_recv()
-                if who == "L":
-                    fars = [pass_on(rows_of("L", 0, 0), "right"), None]
-                elif who == "R":
-                    fars[1] = pass_on(rows_of("R", 0, 1), "left")
-                ref = rows_of(who, 0, half)
-                below_from[who, half] = pass_on(ref, "up")
-                up_from[who, half] = pass_on(ref, "below")
-                cores.append(pass_on(ref, "core"))
-            half = rows // 2
-            a_left.wait_recv()
-            far_upper = pass_on(out.at[o["L"], 0, pl.ds(0, half)], "right")
-            cores.append(pass_on(out.at[o["L"], 0], "core"))
-            a_right.wait_recv()
-            far_lower = pass_on(out.at[o["R"], 0, pl.ds(half, half)], "left")
-            cores.append(pass_on(out.at[o["R"], 0], "core"))
+                return out.at[o[who], m, pl.ds(pl.multiple_of(q[share] * n + first, 16), many)]
+
+            firsts = {}
+            for m, ref in enumerate((g_ref, u_ref)):
+                src, dst = ref.at[pl.ds(mine, n)], out.at[s, m, pl.ds(mine, n)]
+                firsts[m, "L"], firsts[m, "R"] = put(src, dst, "right"), put(src, dst, "left")
+            cores = [put(ref, out.at[s, m], "core") for m, ref in enumerate((g_ref, u_ref))]
+            up_from, below_from, late = {}, {}, []
+            for m in range(2):
+                for who, half in (("L", None), ("R", None), ("F", 0), ("F", 1)):
+                    firsts[(m, who) if half is None else (m, who, half)].wait_recv()
+                    if who == "L":
+                        firsts[m, "F", 0] = pass_on(rows_of(m, "L", 0, 0), "right")
+                    elif who == "R":
+                        firsts[m, "F", 1] = pass_on(rows_of(m, "R", 0, 1), "left")
+                    ref = rows_of(m, who, 0, half)
+                    below_from[m, who, half] = pass_on(ref, "up")
+                    up_from[m, who, half] = pass_on(ref, "below")
+                    cores.append(pass_on(ref, "core"))
             for c in loads:
                 c.wait()
             store = pltpu.make_async_copy(buf, out.at[s], local.at[2])
             store.start()
-            for who, part in (("L", None), ("R", None), ("F", 0), ("F", 1)):
-                below_from[who, part].wait_recv()
-                ref = rows_of(who, -1, part)
-                if (who, part) in (("L", None), ("F", 0)):
-                    late.append((pass_on(ref, "up"), rows_of(who, 2, part)))
-                cores.append(pass_on(ref, "core"))
-                up_from[who, part].wait_recv()
-                ref = rows_of(who, 1, part)
-                if (who, part) in (("R", None), ("F", 1)):
-                    late.append((pass_on(ref, "below"), rows_of(who, 2, part)))
-                cores.append(pass_on(ref, "core"))
+            for m in range(2):
+                for who, part in (("L", None), ("R", None), ("F", 0), ("F", 1)):
+                    below_from[m, who, part].wait_recv()
+                    ref = rows_of(m, who, -1, part)
+                    if (who, part) in (("L", None), ("F", 0)):
+                        late.append((pass_on(ref, "up"), rows_of(m, who, 2, part)))
+                    cores.append(pass_on(ref, "core"))
+                    up_from[m, who, part].wait_recv()
+                    ref = rows_of(m, who, 1, part)
+                    if (who, part) in (("R", None), ("F", 1)):
+                        late.append((pass_on(ref, "below"), rows_of(m, who, 2, part)))
+                    cores.append(pass_on(ref, "core"))
             for c, ref in late:
                 c.wait_recv()
                 cores.append(pass_on(ref, "core"))
-            far_upper.wait_recv()
-            cores.append(pass_on(out.at[o["F"], 0, pl.ds(0, half)], "core"))
-            far_lower.wait_recv()
-            cores.append(pass_on(out.at[o["F"], 0, pl.ds(half, half)], "core"))
             for c in cores:
                 c.wait_recv()
             for c in used:
@@ -374,12 +365,12 @@
             cost_estimate=cost(2 * t * d * ff, 2 * t * ff),
         )(first[None], actt, dy)
 
-    def by_gate_up(dy, at, w, s1, s2, terms=None):
+    def by_gate_up(dy, at, w, s1, s2, first, blocks, terms=None, chunks=None, slots=None, number=None):
         t, d = dy.shape
         share = d // ns
-        ff = s1.shape[1]
+        ff = blocks * WIDE
         r = 512
-        work = Summing(terms[0], 5) if terms else None
+        work = Summing(terms[0], chunks) if terms else None
 
         def kernel(*refs):
             if work:
@@ -397,19 +388,22 @@
                 if work:
                     work.start()
 
+            def turn(at_slot):
+                if work and at_slot in slots:
+                    work.step(len(slots) * j + slots.index(at_slot))
+
             for k in range(0, t, r):
                 rows = slice(k, k + r)
                 back = lax.dot_general(dy_ref[rows, :], w_ref[...], NT, preferred_element_type=f32).astype(bf16).astype(f32)
                 dg[rows, :] = (back * s2_ref[rows, :]).astype(bf16)
                 du[rows, :] = (back * s1_ref[rows, :]).astype(bf16)
+                turn(k // r)
 
             @pl.when(j == 0)
             def _():
                 load.wait()
 
             for k, ref in enumerate((dg, du)):
-                if work:
-                    work.step(2 * j + k)
                 term = jnp.dot(at_ref[...], ref[...], preferred_element_type=f32).astype(bf16)
                 to = slice(k * share, (k + 1) * share)
                 for p in range(ns):
@@ -420,65 +414,73 @@
                         mine[p, to] = block
                     else:
                         theirs[p - nx, to] = block
+                turn(t // r + k)
 
             if work:
-                assert work.last < 2 * (ff // WIDE)
-
-                @pl.when(j == ff // WIDE - 1)
+                @pl.when(j == blocks - 1)
                 def _():
+                    def rest(i, _):
+                        work.step(i)
+                        return 0
+
+                    lax.fori_loop(blocks * len(slots), work.last + 1, rest, 0)
                     work.finish()
 
-        cols = lambda n: pl.BlockSpec((n, WIDE), lambda j: (0, j))
+        cols = lambda n: pl.BlockSpec((n, WIDE), lambda j: (0, first + j))
+        own = lambda n: pl.BlockSpec((n, WIDE), lambda j: (0, j))
         many, parts = (2, nx) if work else (1, ns)
         block = pl.BlockSpec((parts, 2 * share, WIDE), lambda j: (0, 0, j))
         shape = jax.ShapeDtypeStruct
         return pl.pallas_call(
             kernel,
-            grid=(ff // WIDE,),
+            grid=(blocks,),
             name="by_gate_up",
-            in_specs=[whole((t, d)), pl.BlockSpec(memory_space=pl.ANY), pl.BlockSpec((WIDE, d), lambda j: (j, 0)), cols(t), cols(t)] + (work.in_specs if work else []),
-            out_specs=[cols(t), cols(t)] + [block] * many + ([work.out_spec] if work else []),
+            in_specs=[whole((t, d)), pl.BlockSpec(memory_space=pl.ANY), pl.BlockSpec((WIDE, d), lambda j: (first + j, 0)), cols(t), cols(t)] + (work.in_specs if work else []),
+            out_specs=[own(t), own(t)] + [block] * many + ([work.out_spec] if work else []),
             out_shape=[shape((t, ff), bf16)] * 2 + [shape((parts, 2 * share, ff), bf16)] * many + ([work.out_shape] if work else []),
             scratch_shapes=[pltpu.VMEM((d, t), bf16), pltpu.SemaphoreType.DMA(())] + (work.scratch if work else []),
-            compiler_params=params(collective_id=1, has_side_effects=True) if work else params(),
+            compiler_params=params(collective_id=number, has_side_effects=True) if work else params(),
             cost_estimate=cost(6 * t * d * ff, 12 * t * ff),
         )(dy, at, w, s1, s2, *(terms or ()))
 
-    def by_input(dg, du, pair, h, dy, terms=None):
+    def by_input(dgs, dus, pair, h, dy, terms=None):
         t, d = h.shape
-        ff = dg.shape[1]
+        ff = pair.shape[-1]
         share = d // ns
+        many = len(dgs)
         r = 256
         steps = t // r
         work = Summing(terms[0], 8) if terms else None
 
         def kernel(*refs):
+            dg_refs, du_refs, refs = refs[:many], refs[many : 2 * many], refs[2 * many :]
             if work:
-                dg_ref, du_ref, wg_ref, wu_ref, h_ref, dy_ref, m_ref, t_ref, o_ref, out, *scratch = refs
+                wg_ref, wu_ref, h_ref, dy_ref, m_ref, t_ref, o_ref, out, *scratch = refs
                 work.bind(m_ref, t_ref, out, scratch)
 
                 @pl.when(pl.program_id(0) == 0)
                 def _():
                     work.start()
             else:
-                dg_ref, du_ref, wg_ref, wu_ref, h_ref, dy_ref, o_ref = refs
-            da = sum(
-                lax.dot_general(x[...], w[...].reshape(d, ff), NT, preferred_element_type=f32) for x, w in ((dg_ref, wg_ref), (du_ref, wu_ref))
-            )
+                wg_ref, wu_ref, h_ref, dy_ref, o_ref = refs
+            da, k = 0, 0
+            for dg_ref, du_ref in zip(dg_refs, du_refs, strict=True):
+                n = dg_ref.shape[1]
+                for x, w in ((dg_ref, wg_ref), (du_ref, wu_ref)):
+                    da += lax.dot_general(x[...], w[:, :, k : k + n].reshape(d, n), NT, preferred_element_type=f32)
+                if work and k == 0:
+                    work.step(2 * pl.program_id(0))
+                k += n
             wide = h_ref[...].astype(f32)
             scale = lax.rsqrt(jnp.mean(wide * wide, -1, keepdims=True) + EPS)
             back = scale * (da - wide * (scale * scale * jnp.mean(da * wide, -1, keepdims=True)))
             o_ref[...] = (dy_ref[...].astype(f32) + back).astype(bf16)
             if work:
-                work.step(pl.program_id(0))
+                assert work.last < 2 * steps
+                work.step(2 * pl.program_id(0) + 1)
 
                 @pl.when(pl.program_id(0) == steps - 1)
                 def _():
-                    def rest(i, _):
-                        work.step(i)
-                        return 0
-
-                    lax.fori_loop(steps, work.last + 1, rest, 0)
                     work.finish()
 
         rows = lambda n: pl.BlockSpec((r, n), lambda i: (i, 0))
@@ -488,18 +490,18 @@
             kernel,
             grid=(steps,),
             name="by_input",
-            in_specs=[rows(ff)] * 2 + [matrix(0), matrix(1)] + [rows(d)] * 2 + (work.in_specs if work else []),
+            in_specs=[rows(a.shape[1]) for a in (*dgs, *dus)] + [matrix(0), matrix(1)] + [rows(d)] * 2 + (work.in_specs if work else []),
             out_specs=[rows(d), work.out_spec] if work else rows(d),
             out_shape=[shape, work.out_shape] if work else shape,
             scratch_shapes=work.scratch if work else [],
-            compiler_params=params(collective_id=2, has_side_effects=True) if work else params(),
+            compiler_params=params(collective_id=3, has_side_effects=True) if work else params(),
             cost_estimate=cost(4 * t * d * ff, 4 * t * ff),
-        )(dg, du, pair, pair, h, dy, *(terms or ()))
+        )(*dgs, *dus, pair, pair, h, dy, *(terms or ()))
 
     def step(x, dy, *weights):
         layers, share, _ = weights[0].shape
         h, dy = x[0], dy[0]
-        summed = lambda term: lax.psum(lax.psum_scatter(term, "s", scatter_dimension=0, tiled=True), "r")
+        scattered = lambda term: lax.psum_scatter(term, "s", scatter_dimension=0, tiled=True)
         whole_of = lambda w: lax.all_gather(w, "s", axis=0, tiled=True)
 
         kept = []
@@ -514,18 +516,26 @@
             kept.append((h, s1, s2, actt, at, pair, wd))
             if number < layers - 1:
                 h = down(h, act, wd)
-        grads = [None] * layers
+        grads, waiting = [None] * layers, {}
         for number in reversed(range(layers)):
             h, s1, s2, actt, at, pair, wd = kept[number]
-            down_terms = by_down(actt, dy, number == 0)
+            terms = by_down(actt, dy, number == 0)
             if number == 0:
-                dg, du, *terms, g_down = by_gate_up(dy, at, wd, s1, s2, down_terms)
-                dy, g_pair = by_input(dg, du, pair, h, dy, terms)
+                early, late = FIRST, pair.shape[-1] // WIDE - FIRST
+                dg_a, du_a, *terms_a, g_down = by_gate_up(dy, at, wd, s1, s2, 0, early, terms, 5, (1, 4, 5), 1)
+                terms_a, waiting = lax.optimization_barrier((terms_a, waiting))
+                for n, sums in waiting.items():
+                    down_sum, pair_sum = lax.psum(sums, "r")
+                    grads[n] = (pair_sum[:share], pair_sum[share:], down_sum)
+                dg_b, du_b, *terms_b, g_a = by_gate_up(dy, at, wd, s1, s2, early, late, terms_a, 8, (0, 1, 2, 3, 4, 5), 2)
+                dy, g_b = by_input((dg_a, dg_b), (du_a, du_b), pair, h, dy, terms_b)
+                g_pair = jnp.concatenate([g_a, g_b], -1)
+                grads[number] = (g_pair[:share], g_pair[share:], g_down)
             else:
-                dg, du, terms = by_gate_up(dy, at, wd, s1, s2)
-                dy = by_input(dg, du, pair, h, dy)
-                g_down, g_pair = (summed(v) for v in (down_terms, terms.reshape(2 * share * ns, -1)))
-            grads[number] = (g_pair[:share], g_pair[share:], g_down)
+                down_sum = scattered(terms)
+                dg, du, terms = by_gate_up(dy, at, wd, s1, s2, 0, pair.shape[-1] // WIDE)
+                dy = by_input((dg,), (du,), pair, h, dy)
+                waiting[number] = (down_sum, scattered(terms.reshape(2 * share * ns, -1)))
         return (dy[None], *(jnp.stack([g[i] for g in grads]) for i in range(3)))
 
     states, cut = P(("rep", "r", "s"), None, None), P(None, "s", None)

time: 438 us -> 469 us (1.071)
  the two profiles are of different devices: /device:TPU:97 before, /device:TPU:96 now
where the time goes in v2:
time: 469 us; the launch traced here: 462 us
  Pallas kernels  430 us (92%)
  between operations  14.8 us (3%)
  local copies, waits for them, and re-layouts  10.6 us (2%)
    pallas_call x3, Pallas kernels, by_gate_up(): pl.pallas_call(kernel, grid=(blocks,), name='by_gate_up', in_specs=[whole...  173 us
    pallas_call x2, Pallas kernels, by_input(): pl.pallas_call(kernel, grid=(steps,), name='by_input', in_specs=[rows(a.s...  86.5 us
    pallas_call x2, Pallas kernels, gate_up(): pl.pallas_call(kernel, grid=(steps,), name='gate_up', in_specs=[rows(d),...  75 us
    pallas_call x1, Pallas kernels, fetched(): pl.pallas_call(kernel, name='fetched', in_specs=[anywhere] * 2, out_specs...  48 us
    pallas_call x2, Pallas kernels, by_down(): pl.pallas_call(kernel, name='by_down', grid_spec=pltpu.PrefetchScalarGrid...  31.8 us
    pallas_call x1, Pallas kernels, down(): pl.pallas_call(kernel, grid=(t // r,), name='down', in_specs=[rows(d), ro...  16.3 us
  transfers between devices with their start and end apart: 6, of which 0 were waited for; matrix products, arithmetic and copies ran while one was open for 1% of the time, Pallas kernels for 93%

profile of v2, /device:TPU:96, one launch (start us, length us, event | category | flops | bytes accessed | tf_op | source)
XLA Modules:
  0.0 461.6 jit_solution(14315238061574507771)
XLA Ops:
  7.2 0.1 all-gather.8.cloned.1.call-start
  7.3 2.6 fusion
  9.9 0.1 all-gather.6.cloned.1.call-start
  10.0 1.3 slice_bitcast_fusion.4
  11.3 1.1 pad_maximum_fusion
  12.5 0.1 all-gather.10.cloned.1.call-start
  12.6 0.7 all-gather.10.cloned.1.call-update
  13.3 0.1 reduce-scatter.3.cloned.1.call-start
  13.4 48.0 %fetched.1.pair_ref.refs_4_.refs_5_ = bf16[8,2,128,2560]{3,2,1,0:T(8,128)(2,1)} custom-call(bf16[128,2560]{1,0:T(8,128)(2,1)} %get-tuple-element.76.g_ref, bf16[128,2560]{1,0:T(8,128)(2,1)} %get-tuple-element.75.u_ref), custom_call_target="tpu_custom_call" | custom-call | flops 20000000000 | bytes 10485760 | tf_op jit(solution)/shard_map/fetched/pallas_call | solution.py:239
  61.4 37.4 %gate_up.2 = (f32[2048,2560]{1,0:T(8,128)}, f32[2048,2560]{1,0:T(8,128)}, bf16[2048,2560]{1,0:T(8,128)(2,1)}, bf16[2560,2048]{1,0:T(8,128)(2,1)}, bf16[1024,2048]{1,0:T(8,128)(2,1)}) custom-call(bf16[2048,1024]{1,0:T(8,128)(2,1)} %bitcast.40, bf16[8,2,128,2560]{3,2,1,0:T(8,128)(2,1)} %fetched.1.pair_ref.refs_4_.refs_5_), custom_call_target="tpu_custom_call" | custom-call | flops 21474836480 | bytes 73400320 | tf_op jit(solution)/shard_map/gate_up/pallas_call | solution.py:297
  98.8 16.3 %down.1.h_ref.refs_4_ = bf16[2048,1024]{1,0:T(8,128)(2,1)} custom-call(bf16[2048,1024]{1,0:T(8,128)(2,1)} %bitcast.41, bf16[2048,2560]{1,0:T(8,128)(2,1)} %get-tuple-element.34.act_ref, bf16[2560,1024]{1,0:T(8,128)(2,1)} %bitcast.27), custom_call_target="tpu_custom_call" | custom-call | flops 10737418240 | bytes 10485760 | tf_op jit(solution)/shard_map/down/pallas_call | solution.py:319
  115.1 37.6 %gate_up.3 = (f32[2048,2560]{1,0:T(8,128)}, f32[2048,2560]{1,0:T(8,128)}, bf16[2048,2560]{1,0:T(8,128)(2,1)}, bf16[2560,2048]{1,0:T(8,128)(2,1)}, bf16[1024,2048]{1,0:T(8,128)(2,1)}) custom-call(bf16[2048,1024]{1,0:T(8,128)(2,1)} %down.1.h_ref.refs_4_, bf16[8,2,128,2560]{3,2,1,0:T(8,128)(2,1)} %bitcast.33), custom_call_target="tpu_custom_call" | custom-call | flops 21474836480 | bytes 73400320 | tf_op jit(solution)/shard_map/gate_up/pallas_call | solution.py:297
  152.7 15.7 %by_down.3 = bf16[2560,1024]{1,0:T(8,128)(2,1)} custom-call(s32[1]{0:T(128)} %constant.19.clone.1.pos, bf16[2560,2048]{1,0:T(8,128)(2,1)} %get-tuple-element.49.actt_ref, bf16[2048,1024]{1,0:T(8,128)(2,1)} %bitcast.37), custom_call_target="tpu_custom_call" | custom-call | flops 10737418240 | bytes 10485760 | tf_op jit(solution)/shard_map/by_down/pallas_call | solution.py:354
  168.4 0.1 reduce-scatter.5.cloned.1.call-start
  168.5 46.4 %by_gate_up.3 = (bf16[2048,2560]{1,0:T(8,128)(2,1)}, bf16[2048,2560]{1,0:T(8,128)(2,1)}, bf16[8,256,2560]{2,1,0:T(8,128)(2,1)}) custom-call(bf16[2048,1024]{1,0:T(8,128)(2,1)} %bitcast.38, bf16[1024,2048]{1,0:T(8,128)(2,1)} %get-tuple-element.35.refs_1_, bf16[2560,1024]{1,0:T(8,128)(2,1)} %bitcast.36, f32[2048,2560]{1,0:T(8,128)} %get-tuple-element.36.refs_3_, ...), custom_call_target="tpu_custom_call" | custom-call | flops 32212254720 | bytes 62914560 | tf_op jit(solution)/shard_map/by_gate_up/pallas_call | solution.py:434
  215.0 0.1 all-reduce.3.cloned.1.call-start
  215.1 31.5 %by_input.2.dy_ref.refs_0_.refs_7_ = bf16[2048,1024]{1,0:T(8,128)(2,1)} custom-call(bf16[2048,2560]{1,0:T(8,128)(2,1)} %get-tuple-element.38.refs_0_, bf16[2048,2560]{1,0:T(8,128)(2,1)} %get-tuple-element.39.refs_1_, bf16[8,2,128,2560]{3,2,1,0:T(8,128)(2,1)} %bitcast.34, bf16[8,2,128,2560]{3,2,1,0:T(8,128)(2,1)} %bitcast.35, ...), custom_call_target="tpu_custom_call" | custom-call | flops 21474836480 | bytes 20971520 | tf_op jit(solution)/shard_map/by_input/pallas_call | solution.py:489
  246.6 16.2 %by_down.2 = (bf16[4,320,1024]{2,1,0:T(8,128)(2,1)}, bf16[4,320,1024]{2,1,0:T(8,128)(2,1)}) custom-call(s32[1]{0:T(128)} %bitcast.9.pos, bf16[2560,2048]{1,0:T(8,128)(2,1)} %get-tuple-element.43.actt_ref, bf16[2048,1024]{1,0:T(8,128)(2,1)} %by_input.2.dy_ref.refs_0_.refs_7_), custom_call_target="tpu_custom_call" | custom-call | flops 10737418240 | bytes 10485760 | tf_op jit(solution)/shard_map/by_down/pallas_call | solution.py:354
  262.8 57.8 %by_gate_up.4 = (bf16[2048,1536]{1,0:T(8,128)(2,1)}, bf16[2048,1536]{1,0:T(8,128)(2,1)}, bf16[4,256,1536]{2,1,0:T(8,128)(2,1)}, bf16[4,256,1536]{2,1,0:T(8,128)(2,1)}, bf16[320,1024]{1,0:T(8,128)(2,1)}) custom-call(bf16[2048,1024]{1,0:T(8,128)(2,1)} %by_input.2.dy_ref.refs_0_.refs_7_, bf16[1024,2048]{1,0:T(8,128)(2,1)} %get-tuple-element.40.refs_1_, ...), custom_call_target="tpu_custom_call" | custom-call | flops 19327352832 | bytes 37748736 | tf_op jit(solution)/shard_map/by_gate_up/pallas_call | solution.py:434
  320.6 0.1 all-reduce.3.cloned.1.call-update
  320.7 68.3 %by_gate_up.5 = (bf16[2048,1024]{1,0:T(8,128)(2,1)}, bf16[2048,1024]{1,0:T(8,128)(2,1)}, bf16[4,256,1024]{2,1,0:T(8,128)(2,1)}, bf16[4,256,1024]{2,1,0:T(8,128)(2,1)}, bf16[256,1536]{1,0:T(8,128)(2,1)}) custom-call(bf16[2048,1024]{1,0:T(8,128)(2,1)} %by_input.2.dy_ref.refs_0_.refs_7_, bf16[1024,2048]{1,0:T(8,128)(2,1)} %get-tuple-element.40.refs_1_, ...), custom_call_target="tpu_custom_call" | custom-call | flops 12884901888 | bytes 25165824 | tf_op jit(solution)/shard_map/by_gate_up/pallas_call | solution.py:434
  389.0 55.0 %by_input.3 = (bf16[2048,1024]{1,0:T(8,128)(2,1)}, bf16[256,1024]{1,0:T(8,128)(2,1)}) custom-call(bf16[2048,1536]{1,0:T(8,128)(2,1)} %get-tuple-element.46.refs_0_, bf16[2048,1024]{1,0:T(8,128)(2,1)} %get-tuple-element.53.refs_1_, bf16[2048,1536]{1,0:T(8,128)(2,1)} %get-tuple-element.54.refs_2_, bf16[2048,1024]{1,0:T(8,128)(2,1)} %get-tuple-element.55.refs_3_, ...), custom_call_target="tpu_custom_call" | custom-call | flops 21474836480 | bytes 20971520 | tf_op jit(solution)/shard_map/by_input/pallas_call | solution.py:489
  444.0 1.2 constant_dynamic-update-slice_fusion.1
  445.2 1.1 constant_dynamic-update-slice_fusion
  446.2 0.1 slice_bitcast_fusion.1
  446.4 1.4 slice_bitcast_fusion
  447.8 0.1 copy-done.4
  447.9 1.2 pad_maximum_fusion.3
  449.1 1.2 pad_maximum_fusion.2
  450.3 1.2 pad_maximum_fusion.1
  451.5 0.8 copy-done
  452.3 2.0 copy.13
  (18 shorter events, 0.3 us)
Async XLA Ops:
  7.2 2.8 copy-start.2
  7.2 2.8 copy-start.1
  7.2 91.6 %all-gather.8.cloned.1.call-start = ((), (), s32[]{:S(2)}) async-start(), calls=%async_computation.5 | async-start | bytes 5898240 | tf_op jit(solution)/shard_map/all_gather | solution.py:505
  9.9 105.1 %all-gather.6.cloned.1.call-start = ((), (), s32[]{:S(2)}) async-start(), calls=%async_computation.2 | async-start | bytes 11796480 | tf_op jit(solution)/shard_map/all_gather | solution.py:505
  12.5 156.0 %all-gather.10.cloned.1.call-start = ((), (), s32[]{:S(2)}) async-start(), calls=%async_computation.6 | async-start | bytes 5898240 | tf_op jit(solution)/shard_map/all_gather | solution.py:505
  13.3 307.3 %reduce-scatter.3.cloned.1.call-start = ((), (), s32[]{:S(2)}) async-start(), calls=%async_computation.3 | async-start | bytes 5898240 | tf_op jit(solution)/shard_map/reduce_scatter | solution.py:504
  168.4 152.2 %reduce-scatter.5.cloned.1.call-start = ((), (), s32[]{:S(2)}) async-start(), calls=%async_computation.4 | async-start | bytes 11796480 | tf_op jit(solution)/shard_map/reduce_scatter | solution.py:504
  215.0 231.3 %all-reduce.3.cloned.1.call-start = ((), (), s32[]{:S(2)}) async-start(), calls=%async_computation.7 | async-start | bytes 3932160 | tf_op jit(solution)/shard_map/psum | solution.py:528
  446.2 1.6 copy-start.3
  446.4 1.6 copy-start.4
  449.1 3.1 copy-start
Sparse Core Ops, SparseCore 0:
  10.1 44.2 all-gather.7
  56.5 54.1 all-gather.5
  112.3 33.8 all-gather.9
  168.6 37.2 reduce-scatter.2
  215.2 59.6 reduce-scatter.4
  320.8 63.8 all-reduce.2
